TPU v7x, 32 devices: a whole 2x2x4 slice. The times are simulated.
32 devices in a mesh: dp: 8 (over z, core), vocab: 4 (over y, x).
Axes of the slice: x: 2, y: 2, z: 4, core: 2. Of those that a mesh axis runs over, the one named last changes fastest.
Arguments:
- hidden: bfloat16 [384, 5120], P('dp')
- head_weight: bfloat16 [32768, 5120], P(('dp', 'vocab'))
- target_ids: int32 [384], P('dp'), may hold values from 0 to 32767
- response_mask: int32 [384], P('dp'), may hold values 0 or 1
- advantages: bfloat16 [384], P('dp'), may hold values from -0.23925781 to 0.23925781
- seq_tokens: int32 [64], P('dp'), may hold values from 24 to 144
- layer_grads: float32 [8, 512, 4096], P('dp', None, 'vocab'), may hold values from -3 to 3
Outputs:
- grad_hidden: bfloat16 [384, 5120], P('dp', 'vocab')
- grad_weight: bfloat16 [32768, 5120], P(('dp', 'vocab'))
- reduced_bucket: float32 [512, 4096], P('dp', 'vocab')
All inputs are finite; a program needn't handle non-finite values. No bound on the sum of `response_mask` on one device may be relied on, other than what follows from the above.
Results may differ from a plain program's by a relative error of at most 0.015.
Values may be sent and summed in bfloat16 or wider, within the bound.
A program may use at most 192 MiB of HBM per device.

v0:
```python
import jax
import jax.numpy as jnp
from jax import lax
from jax.sharding import PartitionSpec as P

loss_scale = 16.0
entropy_coef = 0.1


def on_device(hidden, head_weight, target_ids, response_mask, advantages, seq_tokens, layer_grads):
    vocab_count = lax.axis_size("vocab")
    voc_rows = head_weight.shape[0]
    bucket_part = lax.psum_scatter(
        layer_grads[0].astype(jnp.bfloat16), "dp", scatter_dimension=0, tiled=True
    ).astype(jnp.float32)
    gathered, adv_all = (
        lax.all_gather(hidden, "dp", axis=0, tiled=True),
        lax.all_gather(advantages, "dp", axis=0, tiled=True),
    )
    labels = lax.all_gather(jnp.stack([target_ids, response_mask]), "dp", axis=1, tiled=True)
    tokens = gathered.shape[0]
    logits = lax.dot_general(
        head_weight, gathered, (((1,), (1,)), ((), ())), preferred_element_type=jnp.float32
    )
    first_id = (lax.axis_index("dp") * vocab_count + lax.axis_index("vocab")) * voc_rows
    vocab_ids = first_id + jnp.arange(voc_rows, dtype=jnp.int32)[:, None]
    onehot_mask = vocab_ids == labels[0][None, :]
    local_max = jnp.max(logits, axis=0)
    shifted = jnp.exp(logits - local_max[None, :])
    local_sum = jnp.sum(shifted, axis=0)
    local_ent = jnp.sum(shifted * logits, axis=0)
    local_tgt = jnp.sum(jnp.where(onehot_mask, logits, jnp.zeros_like(logits)), axis=0)
    count_local = jnp.sum(seq_tokens).astype(jnp.float32)
    row_max = lax.pmax(local_max, ("dp", "vocab"))
    rescale = jnp.exp(local_max - row_max)
    row_sum, row_ent, row_tgt = lax.psum(
        (local_sum * rescale, local_ent * rescale, local_tgt), ("dp", "vocab")
    )
    token_total = lax.psum(count_local, "dp")
    factor = loss_scale * tokens / token_total
    weights = factor * labels[1].astype(jnp.float32)
    advantage = adv_all.astype(jnp.float32)
    mean_logit = row_ent / row_sum
    softmax = jnp.exp(logits - row_max[None, :]) / row_sum[None, :]
    onehot = onehot_mask.astype(jnp.float32)
    logit_grad = weights[None, :] * (
        -advantage[None, :] * (onehot - softmax)
        + entropy_coef * softmax * (logits - mean_logit[None, :])
    )
    grad_bf = logit_grad.astype(jnp.bfloat16)
    row_sums_part = lax.psum_scatter(
        lax.dot_general(
            grad_bf, head_weight, (((0,), (0,)), ((), ())), preferred_element_type=jnp.float32
        ).astype(jnp.bfloat16),
        "dp",
        scatter_dimension=0,
        tiled=True,
    )
    own_hidden = lax.psum_scatter(row_sums_part, "vocab", scatter_dimension=1, tiled=True).astype(
        jnp.float32
    )
    grad_weight = jnp.dot(grad_bf, gathered, preferred_element_type=jnp.float32).astype(
        jnp.bfloat16
    )
    grad_hidden = own_hidden.astype(jnp.bfloat16)
    reduced_bucket = bucket_part * factor
    return (grad_hidden, grad_weight, reduced_bucket)


def solution(mesh):
    in_specs = (
        P("dp", None),
        P(("dp", "vocab"), None),
        P("dp"),
        P("dp"),
        P("dp"),
        P("dp"),
        P("dp", None, "vocab"),
    )
    out_specs = (P("dp", "vocab"), P(("dp", "vocab"), None), P("dp", "vocab"))
    return jax.shard_map(
        on_device, mesh=mesh, in_specs=in_specs, out_specs=out_specs, check_vma=False
    )
```

profile of v0, /device:TPU:0, one launch (start us, length us, event | category | flops | bytes accessed | tf_op | source)
XLA Modules:
  0.0 237.8 jit_solution(2962326343504258552)
XLA Ops:
  7.2 0.0 all-gather.3.cloned.1.call-start
  7.2 0.7 all-gather.3.cloned.1.call-update
  7.9 0.0 copy-start
  7.9 0.0 copy-start.1
  7.9 0.0 copy-start.2
  7.9 0.0 copy-start.4
  7.9 0.0 copy-start.3
  8.0 0.0 reduce-scatter.8.cloned.1.call-start
  8.0 2.7 %convert_bitcast_fusion = bf16[512,1024]{1,0:T(8,128)(2,1)} fusion(f32[1,512,1024]{2,1,0:T(8,128)} %param.13), kind=kLoop, calls=%fused_computation.6 | loop fusion | flops 524288 | bytes 3145728 | tf_op jit(solution)/shard_map/convert_element_type | solution.py:14
  10.7 0.0 reduce-scatter.8.cloned.1.call-update
  10.8 0.0 reduce-scatter.4.cloned.1.call-start
  10.9 13.5 %all-gather = s32[8,48,2]{1,2,0:T(2,128)S(1)} all-gather(s32[1,48,2]{1,2,0:T(2,128)S(1)} %add_bitcast_fusion), channel_id=1, replica_groups=mesh['dp'=8,'vocab'=4] {'dp'}, dimensions={0}, use_global_device_ids=true | all-gather | bytes 3456 | tf_op jit(solution)/shard_map/all_gather | solution.py:20
  24.4 0.6 reduce_sum.27
  25.6 0.1 reshape.22
  25.7 15.5 %psum.21 = f32[]{:T(128)} all-reduce(f32[]{:T(128)S(6)} %convert_element_type.33), channel_id=1, replica_groups=mesh['dp'=8,'vocab'=4] {'dp'}, use_global_device_ids=true, to_apply=%region_1.0 | all-reduce | flops 1 | bytes 8 | tf_op jit(solution)/shard_map/psum | solution.py:39
  42.0 0.6 dynamic-slice
  43.2 0.2 dynamic-update-slice
  43.5 14.2 %all-reduce = bf16[384]{0:T(512)(128)(2,1)S(1)} all-reduce(bf16[384]{0:T(512)(128)(2,1)S(1)} %dynamic-update-slice), channel_id=1, replica_groups=mesh['dp'=8,'vocab'=4] {'dp'}, use_global_device_ids=true, to_apply=%add | all-reduce | flops 384 | bytes 1536
  57.7 0.0 all-gather.3.cloned.1.call-done
  57.7 9.5 %fusion.5 = (f32[384]{0:T(512)S(1)}, f32[1024,384]{1,0:T(8,128)S(1)}) fusion(bf16[1024,5120]{1,0:T(8,128)(2,1)} %param.8, bf16[384,5120]{1,0:T(8,128)(2,1)} %all-gather.3.cloned.1.call-done), kind=kOutput, calls=%fused_computation.18 | convolution fusion | flops 4026924544 | bytes 15992320 | tf_op jit(solution)/shard_map/dot_general | solution.py:22
  67.2 39.0 %pmax.7 = f32[384]{0:T(512)S(1)} all-reduce(f32[384]{0:T(512)S(1)} %get-tuple-element.9), channel_id=1, replica_groups=mesh['dp'=8,'vocab'=4] {'dp','vocab'}, use_global_device_ids=true, to_apply=%region_3.0 | all-reduce | flops 384 | bytes 3072 | tf_op jit(solution)/shard_map/pmax | solution.py:34
  106.3 0.3 fusion
  106.7 40.6 %all-reduce.1 = (f32[384]{0:T(512)S(1)}, f32[384]{0:T(512)S(1)}) all-reduce(f32[384]{0:T(512)S(1)} %get-tuple-element.8, f32[384]{0:T(512)S(1)} %get-tuple-element.7), channel_id=1, replica_groups=mesh['dp'=8,'vocab'=4] {'dp','vocab'}, use_global_device_ids=true, to_apply=%region_7.0 | all-reduce | flops 768 | bytes 6144 | tf_op jit(solution)/shard_map/psum | solution.py:36
  147.2 10.6 %convolution_convert_fusion.1 = bf16[384,5120]{1,0:T(8,128)(2,1)} fusion(bf16[1024,5120]{1,0:T(8,128)(2,1)} %param.8, f32[1024,384]{1,0:T(8,128)S(1)} %get-tuple-element.10, f32[384]{0:T(512)S(1)} %div.17, f32[384]{0:T(512)S(1)} %get-tuple-element.6, f32[384]{0:T(512)S(1)} %pmax.7, s32[384]{0:T(512)S(1)} %slice_reduce_fusion, ...), kind=kOutput, calls=%fused_computation.1 | convolution fusion | flops 4033216512 | bytes 16004096 | tf_op jit(solution)/shard_map/dot_general | solution.py:52
  157.8 0.0 reduce-scatter.4.cloned.1.call-update
  157.8 0.2 reduce-scatter.6.cloned.1.call-start
  158.0 0.0 reduce-scatter.8.cloned.1.call-done
  158.1 1.6 convert_multiply_fusion
  159.7 45.5 %reduce-scatter.4.cloned.1.call-done = bf16[48,5120]{1,0:T(8,128)(2,1)} async-done(((bf16[384,5120]{1,0:T(8,128)(2,1)}), bf16[48,5120]{1,0:T(8,128)(2,1)}) %reduce-scatter.4.cloned.1.call-update) | async-done | bytes 491536 | tf_op jit(solution)/shard_map/reduce_scatter | solution.py:51
  205.1 0.0 reduce-scatter.6.cloned.1.call-update
  205.2 10.8 %convolution_convert_fusion = bf16[1024,5120]{1,0:T(8,128)(2,1)} fusion(bf16[384,5120]{1,0:T(8,128)(2,1)} %all-gather.3.cloned.1.call-done, f32[1024,384]{1,0:T(8,128)S(1)} %get-tuple-element.10, f32[384]{0:T(512)S(1)} %div.17, f32[384]{0:T(512)S(1)} %get-tuple-element.6, f32[384]{0:T(512)S(1)} %pmax.7, s32[384]{0:T(512)S(1)} %slice_reduce_fusion, ...), kind=kOutput, calls=%fused_computation | convolution fusion | flops 4036493312 | bytes 16004096 | tf_op jit(solution)/shard_map/dot_general | solution.py:62
  215.9 15.3 %reduce-scatter.6.cloned.1.call-done = bf16[48,1280]{1,0:T(8,128)(2,1)} async-done(((bf16[48,5120]{1,0:T(8,128)(2,1)}), bf16[48,1280]{1,0:T(8,128)(2,1)}) %reduce-scatter.6.cloned.1.call-update) | async-done | bytes 122896 | tf_op jit(solution)/shard_map/reduce_scatter | solution.py:59
  (14 shorter events, 0.1 us)
Async XLA Ops:
  7.2 50.5 %all-gather.3.cloned.1.call-start = ((), (), s32[]{:S(2)}) async-start(), calls=%async_computation.3 | async-start | bytes 4423680 | tf_op jit(solution)/shard_map/all_gather | solution.py:17
  7.9 2.9 %copy-start = (s32[48]{0:T(128)S(1)}, s32[48]{0:T(128)}, u32[]{:S(2)}) copy-start(s32[48]{0:T(128)} %param.10) | copy-start | bytes 580
  7.9 2.9 %copy-start.1 = (s32[48]{0:T(128)S(1)}, s32[48]{0:T(128)}, u32[]{:S(2)}) copy-start(s32[48]{0:T(128)} %param.9) | copy-start | bytes 580
  7.9 16.4 %copy-start.2 = (s32[8]{0:T(128)S(1)}, s32[8]{0:T(128)}, u32[]{:S(2)}) copy-start(s32[8]{0:T(128)} %param.12) | copy-start | bytes 100
  7.9 34.0 %copy-start.4 = (u32[32]{0:T(128)S(1)}, u32[32]{0:T(128)}, u32[]{:S(2)}) copy-start(u32[32]{0:T(128)} %constant.26) | copy-start | bytes 388
  7.9 35.3 %copy-start.3 = (bf16[48]{0:T(256)(128)(2,1)S(1)}, bf16[48]{0:T(256)(128)(2,1)}, u32[]{:S(2)}) copy-start(bf16[48]{0:T(256)(128)(2,1)} %param.11) | copy-start | bytes 292
  8.0 150.1 %reduce-scatter.8.cloned.1.call-start = ((), (), s32[]{:S(2)}) async-start(), calls=%async_computation.6 | async-start | bytes 1179648 | tf_op jit(solution)/shard_map/reduce_scatter | solution.py:13
  10.8 194.4 %reduce-scatter.4.cloned.1.call-start = ((), (), s32[]{:S(2)}) async-start(), calls=%async_computation.4 | async-start | bytes 4423680 | tf_op jit(solution)/shard_map/reduce_scatter | solution.py:51
  157.8 73.5 %reduce-scatter.6.cloned.1.call-start = ((), (), s32[]{:S(2)}) async-start(), calls=%async_computation.5 | async-start | bytes 614400 | tf_op jit(solution)/shard_map/reduce_scatter | solution.py:59
Sparse Core Ops, SparseCore 0:
  9.6 47.9 all-gather.2
  59.9 31.6 reduce-scatter.7
  157.9 47.1 reduce-scatter.3
  208.4 22.7 reduce-scatter.5
where the time goes:
time: 238 us
  blocking collectives  123 us (52%)
  waiting for transfers between devices  61.5 us (26%)
  matrix products  30.9 us (13%)
  between operations  15.9 us (7%)
  other arithmetic  5.4 us (2%)
    reduce_scatter x1, waiting for transfers between devices, on_device(): lax.psum_scatter(lax.dot_general(grad_bf, head_weight, (((0,), (0,)), (()...  45.5 us
    psum x1, blocking collectives, on_device(): lax.psum((local_sum * rescale, local_ent * rescale, local_tgt), ('dp', 'v...  40.6 us
    pmax x1, blocking collectives, on_device(): row_max = lax.pmax(local_max, ('dp', 'vocab'))  39 us
    psum x1, blocking collectives, on_device(): token_total = lax.psum(count_local, 'dp')  15.5 us
    reduce_scatter x1, waiting for transfers between devices, on_device(): lax.psum_scatter(row_sums_part, 'vocab', scatter_dimension=1, tiled=True)  15.3 us
    unnamed x1, blocking collectives  14.2 us
    all_gather x1, blocking collectives, on_device(): lax.all_gather(jnp.stack([target_ids, response_mask]), 'dp', axis=1, tile...  13.5 us
    dot_general x1, matrix products, on_device(): jnp.dot(grad_bf, gathered, preferred_element_type=jnp.float32)  10.8 us
  transfers between devices with their start and end apart: 4, of which 2 were waited for; matrix products, arithmetic and copies ran while one was open for 16% of the time, Pallas kernels for 0%

commit v1 on v0

v1 whole, which is shorter than its diff:
```python
import functools
import jax
import jax.numpy as jnp
from jax import lax
from jax.experimental import pallas as pl
from jax.experimental.pallas import tpu as pltpu
from jax.sharding import PartitionSpec as P

loss_scale = 16.0
entropy_coef = 0.1
MESH = pl.DeviceIdType.MESH
F32 = jnp.float32
BF16 = jnp.bfloat16


def kernel(ndp, nv, hid, w_hbm, meta, lg, hid_out, grad_out, gh_out, bk_out, meta_out,
           w, hall, mbuf, logits, grad_t, gh, st_a, st_b, sa, sb, r1, sbuf, r2, own, t, r3,
           lgb, b1, bs, b2, lsem,
           g1s, g1r, pos, por, ms, mr, b1s, b1r, b2s, b2r, g2s, g2r, hps, hpr,
           sas, sar, sbs, sbr, r1s, r1r, r2s, r2r, r3s, r3r):
    rows, depth = hid.shape
    voc = w.shape[0]
    tokens = hall.shape[0]
    nz = ndp // 2
    quart = depth // nv
    brow = lg.shape[0] // ndp
    dp = lax.axis_index("dp")
    v = lax.axis_index("vocab")
    core = lax.rem(dp, 2)
    z = dp // 2
    mate = 2 * z + 1 - core
    pending = []

    def block(d):
        return pl.ds(pl.multiple_of(d * rows, rows), rows)

    def cols(q):
        return pl.ds(pl.multiple_of(q * quart, quart), quart)

    def bblock(d):
        return pl.ds(pl.multiple_of(d * brow, brow), brow)

    def copy(src, dst, s, r, d, q):
        return pltpu.make_async_remote_copy(
            src_ref=src, dst_ref=dst, send_sem=s, recv_sem=r, device_id=(d, q),
            device_id_type=MESH)

    def send(*args):
        c = copy(*args)
        c.start()
        pending.append(c)

    def arrived(ref, s, r):
        copy(ref, ref, s, r, mate, v).wait_recv()

    def zfwd(k):
        return lax.rem(z + k, nz)

    def zback(k):
        return lax.rem(z + nz - k, nz)

    def vfwd(k):
        return lax.rem(v + k, nv)

    def vback(k):
        return lax.rem(v + nv - k, nv)

    wcopy = pltpu.make_async_copy(w_hbm, w, lsem.at[0])
    wcopy.start()
    barrier = pltpu.get_barrier_semaphore()
    for k in range(1, ndp):
        pl.semaphore_signal(barrier, inc=1, device_id=(lax.rem(dp + k, ndp), v), device_id_type=MESH)
    for k in range(1, nv):
        pl.semaphore_signal(barrier, inc=1, device_id=(dp, vfwd(k)), device_id_type=MESH)
    pl.semaphore_wait(barrier, ndp + nv - 2)

    for k in range(1, nz):
        send(hid.at[:, cols(v)], hall.at[block(dp), cols(v)], g1s.at[k - 1], g1r.at[k - 1],
             2 * zfwd(k) + core, v)
    send(hid, hall.at[block(dp), :], pos.at[0], por.at[0], mate, v)
    for k in range(1, ndp):
        send(meta, mbuf.at[k - 1], ms.at[k - 1], mr.at[k - 1], lax.rem(dp + k, ndp), v)
    hall[block(dp), :] = hid[...]
    lgb[...] = lg[...].astype(BF16)
    for k in range(nz):
        send(lgb.at[bblock(2 * k + 1 - core), :], b1.at[pl.ds(k * brow, brow), :],
             b1s.at[k], b1r.at[k], mate, v)
    for k in range(1, nz):
        ref = hall.at[block(2 * zback(k) + core), cols(v)]
        arrived(ref, g1s.at[k - 1], g1r.at[k - 1])
        for j in range(1, nv):
            i = (k - 1) * (nv - 1) + j - 1
            send(ref, ref, g2s.at[i], g2r.at[i], dp, vfwd(j))
        i = (k - 1) * nv
        send(ref, ref, hps.at[i], hpr.at[i], mate, v)
    for k in range(nz):
        arrived(b1.at[pl.ds(k * brow, brow), :], b1s.at[k], b1r.at[k])
    for k in range(1, nz):
        zz = zfwd(k)
        bs[k - 1] = (lg[bblock(2 * zz + core), :] + b1[bblock(zz), :].astype(F32)).astype(BF16)
        send(bs.at[k - 1], b2.at[k - 1], b2s.at[k - 1], b2r.at[k - 1], 2 * zz + core, v)
    bk_out[...] = lg[bblock(dp), :] + b1[bblock(z), :].astype(F32)
    for k in range(1, ndp):
        arrived(mbuf.at[k - 1], ms.at[k - 1], mr.at[k - 1])
    total = meta[...]
    for k in range(1, ndp):
        total = total + mbuf[k - 1]
    meta_out[...] = total
    for k in range(1, nz):
        for j in range(1, nv):
            i = (k - 1) * (nv - 1) + j - 1
            ref = hall.at[block(2 * zback(k) + core), cols(vback(j))]
            arrived(ref, g2s.at[i], g2r.at[i])
            i = (k - 1) * nv + j
            send(ref, ref, hps.at[i], hpr.at[i], mate, v)
    arrived(hall.at[block(mate), :], pos.at[0], por.at[0])
    for k in range(1, nz):
        for j in range(nv):
            i = (k - 1) * nv + j
            ref = hall.at[block(2 * zback(k) + 1 - core), cols(vback(j))]
            arrived(ref, hps.at[i], hpr.at[i])
    hcopy = pltpu.make_async_copy(hall, hid_out, lsem.at[1])
    hcopy.start()
    wcopy.wait()

    vt = 128

    def logits_step(i, top):
        at = pl.ds(pl.multiple_of(i * vt, vt), vt)
        part = lax.dot_general(w[at, :], hall[...], (((1,), (1,)), ((), ())),
                               preferred_element_type=F32)
        logits[at, :] = part
        return jnp.maximum(top, jnp.max(part, axis=0, keepdims=True))

    top = lax.fori_loop(0, voc // vt, logits_step, jnp.full((1, tokens), -jnp.inf, F32))

    def stats_step(i, carry):
        s, e = carry
        part = logits[pl.ds(pl.multiple_of(i * vt, vt), vt), :]
        x = jnp.exp(part - top)
        return (s + jnp.sum(x, axis=0, keepdims=True), e + jnp.sum(x * part, axis=0, keepdims=True))

    zero = jnp.zeros((1, tokens), F32)
    s, e = lax.fori_loop(0, voc // vt, stats_step, (zero, zero))

    def merge(buf, snd, ss, rs, count, target, m, s, e):
        snd[0:1, :] = m
        snd[1:2, :] = s
        snd[2:3, :] = e
        snd[3:8, :] = jnp.zeros((5, tokens), F32)
        for k in range(1, count):
            send(snd, buf.at[k - 1], ss.at[k - 1], rs.at[k - 1], *target(k))
        for k in range(1, count):
            arrived(buf.at[k - 1], ss.at[k - 1], rs.at[k - 1])
        new = m
        for k in range(1, count):
            new = jnp.maximum(new, buf[k - 1, 0:1, :])
        f = jnp.exp(m - new)
        s, e = s * f, e * f
        for k in range(1, count):
            f = jnp.exp(buf[k - 1, 0:1, :] - new)
            s = s + buf[k - 1, 1:2, :] * f
            e = e + buf[k - 1, 2:3, :] * f
        return new, s, e

    m, s, e = merge(st_a, sa, sas, sar, ndp, lambda k: (lax.rem(dp + k, ndp), v), top, s, e)
    m, s, e = merge(st_b, sb, sbs, sbr, nv, lambda k: (dp, vfwd(k)), m, s, e)

    label = total[0:1, :]
    weight = loss_scale * tokens / total[3:4, :] * total[1:2, :]
    adv = total[2:3, :]
    inv = 1.0 / s
    mean = e * inv
    first = (dp * nv + v) * voc

    def grad_step(i, carry):
        at = pl.ds(pl.multiple_of(i * vt, vt), vt)
        part = logits[at, :]
        p = jnp.exp(part - m) * inv
        ids = (first + i * vt + lax.broadcasted_iota(jnp.int32, part.shape, 0)).astype(F32)
        hot = jnp.where(ids == label, 1.0, 0.0)
        g = weight * (-adv * (hot - p) + entropy_coef * p * (part - mean))
        grad_out[at, :] = g.astype(BF16)
        grad_t[:, at] = g.T.astype(BF16)
        return carry

    lax.fori_loop(0, voc // vt, grad_step, 0)

    ct = 256 if quart % 256 == 0 else 128
    for kq in list(range(1, nv)) + [0]:
        q = vfwd(kq)

        def gh_step(i, carry):
            at = pl.ds(pl.multiple_of(q * quart + i * ct, 128), ct)
            gh[:, at] = jnp.dot(grad_t[...], w[:, at], preferred_element_type=F32).astype(BF16)
            return carry

        lax.fori_loop(0, quart // ct, gh_step, 0)
        for k in range(nz):
            i = kq * nz + k
            zz = zfwd(k)
            send(gh.at[block(2 * zz + 1 - core), cols(q)], r1.at[block(zz), cols(q)],
                 r1s.at[i], r1r.at[i], mate, v)
    for k in list(range(1, nz)) + [0]:
        zz = zfwd(k)
        for kq in list(range(1, nv)) + [0]:
            q = vfwd(kq)
            i = kq * nz + k
            arrived(r1.at[block(zz), cols(q)], r1s.at[i], r1r.at[i])
            both = (gh[block(2 * zz + core), cols(q)].astype(F32)
                    + r1[block(zz), cols(q)].astype(F32))
            if kq:
                i = (kq - 1) * nz + k
                sbuf[i] = both.astype(BF16)
                send(sbuf.at[i], r2.at[i], r2s.at[i], r2r.at[i], dp, q)
            else:
                own[k] = both
    for k in list(range(1, nz)) + [0]:
        acc = own[k]
        for j in range(1, nv):
            i = (j - 1) * nz + k
            arrived(r2.at[i], r2s.at[i], r2r.at[i])
            acc = acc + r2[i].astype(F32)
        if k:
            t[k - 1] = acc.astype(BF16)
            send(t.at[k - 1], r3.at[k - 1], r3s.at[k - 1], r3r.at[k - 1], 2 * zfwd(k) + core, v)
        else:
            own[0] = acc
    bsum = bk_out[...]
    for k in range(1, nz):
        arrived(b2.at[k - 1], b2s.at[k - 1], b2r.at[k - 1])
        bsum = bsum + b2[k - 1].astype(F32)
    bk_out[...] = bsum
    acc = own[0]
    for k in range(1, nz):
        arrived(r3.at[k - 1], r3s.at[k - 1], r3r.at[k - 1])
        acc = acc + r3[k - 1].astype(F32)
    gh_out[...] = acc.astype(BF16)
    hcopy.wait()
    for c in pending:
        c.wait_send()


def on_device(ndp, nv, hidden, head_weight, target_ids, response_mask, advantages, seq_tokens, layer_grads):
    rows, depth = hidden.shape
    voc = head_weight.shape[0]
    tokens = rows * ndp
    nz = ndp // 2
    quart = depth // nv
    bucket = layer_grads[0]
    brows, bcols = bucket.shape
    brow = brows // ndp
    small = jnp.stack([target_ids.astype(F32), response_mask.astype(F32), advantages.astype(F32)])
    meta = lax.dynamic_update_slice(jnp.zeros((8, tokens), F32), small,
                                    (jnp.int32(0), lax.axis_index("dp") * rows))
    meta = meta.at[3].set(jnp.sum(seq_tokens).astype(F32))
    vm = pl.BlockSpec(memory_space=pltpu.VMEM)
    hbm = pl.BlockSpec(memory_space=pl.ANY)
    dma = lambda n: pltpu.SemaphoreType.DMA((n,))
    pairs = [nz - 1, 1, ndp - 1, nz, nz - 1, (nz - 1) * (nv - 1), (nz - 1) * nv,
             ndp - 1, nv - 1, nz * nv, nz * (nv - 1), nz - 1]
    gathered, grad_bf, own_hidden, bucket_sum, total = pl.pallas_call(
        functools.partial(kernel, ndp, nv),
        out_shape=(
            jax.ShapeDtypeStruct((tokens, depth), BF16),
            jax.ShapeDtypeStruct((voc, tokens), BF16),
            jax.ShapeDtypeStruct((rows, quart), BF16),
            jax.ShapeDtypeStruct((brow, bcols), F32),
            jax.ShapeDtypeStruct((8, tokens), F32),
        ),
        in_specs=[vm, hbm, vm, vm],
        out_specs=(hbm, vm, vm, vm, vm),
        scratch_shapes=[
            pltpu.VMEM((voc, depth), BF16),
            pltpu.VMEM((tokens, depth), BF16),
            pltpu.VMEM((ndp - 1, 8, tokens), F32),
            pltpu.VMEM((voc, tokens), F32),
            pltpu.VMEM((tokens, voc), BF16),
            pltpu.VMEM((tokens, depth), BF16),
            pltpu.VMEM((ndp - 1, 8, tokens), F32),
            pltpu.VMEM((nv - 1, 8, tokens), F32),
            pltpu.VMEM((8, tokens), F32),
            pltpu.VMEM((8, tokens), F32),
            pltpu.VMEM((nz * rows, depth), BF16),
            pltpu.VMEM((nz * (nv - 1), rows, quart), BF16),
            pltpu.VMEM((nz * (nv - 1), rows, quart), BF16),
            pltpu.VMEM((nz, rows, quart), F32),
            pltpu.VMEM((nz - 1, rows, quart), BF16),
            pltpu.VMEM((nz - 1, rows, quart), BF16),
            pltpu.VMEM((brows, bcols), BF16),
            pltpu.VMEM((nz * brow, bcols), BF16),
            pltpu.VMEM((nz - 1, brow, bcols), BF16),
            pltpu.VMEM((nz - 1, brow, bcols), BF16),
            pltpu.SemaphoreType.DMA((2,)),
        ] + [dma(n) for n in pairs for _ in range(2)],
        compiler_params=pltpu.CompilerParams(
            collective_id=0, has_side_effects=True, vmem_limit_bytes=67043328),
    )(hidden, head_weight, meta, bucket)
    grad_weight = jnp.dot(grad_bf, gathered, preferred_element_type=F32).astype(BF16)
    factor = loss_scale * tokens / total[3, 0]
    return (own_hidden, grad_weight, bucket_sum * factor)


def solution(mesh):
    in_specs = (
        P("dp", None),
        P(("dp", "vocab"), None),
        P("dp"),
        P("dp"),
        P("dp"),
        P("dp"),
        P("dp", None, "vocab"),
    )
    out_specs = (P("dp", "vocab"), P(("dp", "vocab"), None), P("dp", "vocab"))
    body = functools.partial(on_device, mesh.shape["dp"], mesh.shape["vocab"])
    return jax.shard_map(
        body, mesh=mesh, in_specs=in_specs, out_specs=out_specs, check_vma=False
    )
```

time: 238 us -> 109 us (0.46)
  blocking collectives: 123 us -> 0 us
  Pallas kernels: 0 us -> 86.2 us
  waiting for transfers between devices: 61.5 us -> 0 us
  matrix products: 30.9 us -> 10.4 us
  between operations: 15.9 us -> 2 us
  local copies, waits for them, and re-layouts: 0.96 us -> 5.14 us
    pallas_call x0 -> x1, Pallas kernels: none -> 86.2 us  [on_device(): pl.pallas_call(functools.partial(kernel, ndp, nv), out_shape=(jax.ShapeDt...]
    reduce_scatter x3 -> x0, waiting for transfers between devices: 60.8 us -> none  [the longest x1 45.5 us: on_device(): lax.psum_scatter(lax.dot_general(grad_bf, head_weight, (((0,), (0,)), (()...]
    psum x2 -> x0, blocking collectives: 56.1 us -> none  [the longest x1 40.6 us: on_device(): lax.psum((local_sum * rescale, local_ent * rescale, local_tgt), ('dp', 'v...]
    pmax x1 -> x0, blocking collectives: 39 us -> none  [on_device(): row_max = lax.pmax(local_max, ('dp', 'vocab'))]
    dot_general x3 -> x1, matrix products: 30.9 us -> 10.4 us  [on_device(): jnp.dot(grad_bf, gathered, preferred_element_type=F32).astype(BF16)]
    unnamed x1 -> x0, blocking collectives: 14.2 us -> none
    all_gather x1 -> x0, blocking collectives: 13.5 us -> none  [on_device(): lax.all_gather(jnp.stack([target_ids, response_mask]), 'dp', axis=1, tile...]
    convert_element_type x1 -> x0, other arithmetic: 2.74 us -> none  [on_device(): layer_grads[0].astype(jnp.bfloat16)]
  transfers between devices with their start and end apart: 4 -> 0, of which waited for: 2 -> 0; matrix products, arithmetic and copies ran while one was open for 16% -> 0% of each run, Pallas kernels for 0% -> 0%
where the time goes in v1:
time: 109 us; the launch traced here: 108 us
  Pallas kernels  86.2 us (79%)
  matrix products  10.4 us (10%)
  local copies, waits for them, and re-layouts  5.14 us (5%)
  other arithmetic  4.32 us (4%)
  between operations  2 us (2%)
    pallas_call x1, Pallas kernels, on_device(): pl.pallas_call(functools.partial(kernel, ndp, nv), out_shape=(jax.ShapeDt...  86.2 us
    dot_general x1, matrix products, on_device(): jnp.dot(grad_bf, gathered, preferred_element_type=F32).astype(BF16)  10.4 us

profile of v1, /device:TPU:0, one launch (start us, length us, event | category | flops | bytes accessed | tf_op | source)
XLA Modules:
  0.0 108.1 jit_solution(18017931858636286354)
XLA Ops:
  0.6 1.3 %reduce_sum.9 = s32[]{:T(128)} reduce(s32[8]{0:T(128)} %param.14, s32[]{:T(128)} %constant.38.clone.1), dimensions={0}, to_apply=%region_0.0 | reduce | flops 7 | bytes 40 | tf_op jit(solution)/shard_map/reduce_sum | solution.py:256
  2.6 0.7 bitcast_convert_fusion
  3.2 0.7 convert_bitcast_fusion
  3.9 0.6 broadcast_in_dim.4
  4.5 1.4 %dynamic_update_slice.3 = f32[8,384]{1,0:T(8,128)} dynamic-update-slice(f32[8,384]{1,0:T(8,128)} %broadcast_in_dim.4, f32[3,48]{1,0:T(4,128)S(1)} %pad_maximum_fusion, s32[]{:T(128)} %constant.38.clone.1, s32[]{:T(128)S(6)} %select_n.3) | dynamic-update-slice | bytes 1156 | tf_op jit(solution)/shard_map/dynamic_update_slice | solution.py:254
  5.9 1.3 %scatter.4.meta = f32[8,384]{1,0:T(8,128)} dynamic-update-slice(f32[8,384]{1,0:T(8,128)} %dynamic_update_slice.3, f32[1,384]{1,0:T(1,128)S(1)} %broadcast.19, s32[]{:T(128)} %constant.43.clone.1, s32[]{:T(128)} %constant.38.clone.1) | dynamic-update-slice | bytes 3076 | tf_op jit(solution)/shard_map/scatter | solution.py:256
  7.2 86.2 %shard_map.94 = (bf16[384,5120]{1,0:T(8,128)(2,1)}, bf16[1024,384]{1,0:T(8,128)(2,1)}, bf16[48,1280]{1,0:T(8,128)(2,1)}, f32[64,1024]{1,0:T(8,128)}, f32[8,384]{1,0:T(8,128)}) custom-call(bf16[48,5120]{1,0:T(8,128)(2,1)} %hid.1, bf16[1024,5120]{1,0:T(8,128)(2,1)} %w_hbm.1, f32[8,384]{1,0:T(8,128)} %scatter.4.meta, f32[512,1024]{1,0:T(8,128)} %bitcast.11), custom_call_target="tpu_custom_call" | custom-call | tf_op jit(solution)/shard_map/pallas_call | solution.py:262
  93.5 1.2 %slice.18 = f32[1,1]{1,0:T(1,128)} slice(f32[8,384]{1,0:T(8,128)} %get-tuple-element.24), slice={[3:4], [0:1]} | slice | bytes 8 | tf_op jit(solution)/shard_map/slice | solution.py:300
  95.4 1.7 %broadcast_multiply_fusion = f32[64,1024]{1,0:T(8,128)} fusion(f32[64,1024]{1,0:T(8,128)} %get-tuple-element.23, f32[]{:T(128)} %bitcast.4), kind=kLoop, calls=%fused_computation.1 | loop fusion | flops 65536 | bytes 524292 | tf_op jit(solution)/shard_map/mul | solution.py:301
  97.0 0.0 copy-start
  97.0 10.4 %convolution_convert_fusion = bf16[1024,5120]{1,0:T(8,128)(2,1)} fusion(bf16[1024,384]{1,0:T(8,128)(2,1)} %get-tuple-element.21, bf16[384,5120]{1,0:T(8,128)(2,1)} %get-tuple-element.22), kind=kOutput, calls=%fused_computation | convolution fusion | flops 4031774720 | bytes 15204352 | tf_op jit(solution)/shard_map/dot_general | solution.py:299
  107.5 0.0 copy-done
  107.5 0.6 copy.13
  (2 shorter events, 0.0 us)
Async XLA Ops:
  97.0 10.4 %copy-start = (bf16[48,1280]{1,0:T(8,128)(2,1)S(1)}, bf16[48,1280]{1,0:T(8,128)(2,1)}, u32[]{:S(2)}) copy-start(bf16[48,1280]{1,0:T(8,128)(2,1)} %get-tuple-element.30) | copy-start | bytes 368644
